TPU v7x, 32 devices: a whole 2x2x4 slice. The times are simulated.
32 devices in a mesh: groups: 1, ep: 16 (over z, y, x), hp: 2 (over core).
Axes of the slice: x: 2, y: 2, z: 4, core: 2. Of those that a mesh axis runs over, the one named last changes fastest.
Arguments:
- x_pre: bfloat16 [896, 1536], P(('groups', 'ep')), may hold values from -6 to 6
- x_dec: bfloat16 [128, 1536], P(('groups', 'ep')), may hold values from -6 to 6
- prefill_query_rows: bfloat16 [896, 2048], P(('groups', 'ep'), 'hp'), may hold values from -240 to 240
- prefill_key_values: bfloat16 [2, 896, 256], P(None, ('groups', 'ep'), 'hp'), may hold values from -6.1 to 6.1
- decode_query_rows: bfloat16 [128, 2048], P(('groups', 'ep'), 'hp'), may hold values from -240 to 240
- decode_key_values: bfloat16 [2, 128, 256], P(None, ('groups', 'ep'), 'hp'), may hold values from -6 to 6
- cache: bfloat16 [2, 128, 128, 256], P(None, ('groups', 'ep'), None, 'hp'), may hold values from -6.1 to 6.1
- cache_len: int32 [128], P(('groups', 'ep')), may hold values from 2 to 128
- sinks: float32 [32], P('hp'), may hold values from -1 to 5
- o_weight: bfloat16 [2048, 1536], P('hp', 'ep'), may hold values from -0.125 to 0.125
- norm_gain: float32 [1536], replicated, may hold values from 0.5 to 1.5
- expert_ids: int32 [1024, 4], P(('groups', 'ep')), may hold values from 0 to 7, all different within a row; in each aligned block of 64 rows (0 to 63, 64 to 127, ...) at most 48 rows name the same one
- route_logits: float32 [1024, 4], P(('groups', 'ep')), may hold values from -6 to 6
- w_gate_up: bfloat16 [16, 2, 1536, 768], P('ep', None, None, 'hp'), may hold values from -0.15625 to 0.15625
- w_down: bfloat16 [16, 768, 1536], P('ep', 'hp'), may hold values from -0.15625 to 0.15625
Outputs:
- layer_out: bfloat16 [1024, 1536], P(('groups', 'ep', 'hp'))
Inputs may be any that keep to these rules, and one draw needn't show every extreme that they name: `expert_ids`: each row names 4 different experts; among the rows of one index of ep no expert is named by more than 48 rows, and in every draw some expert is named by exactly 48 rows of some index.
All inputs are finite; a program needn't handle non-finite values.
Results may differ from a plain program's by a relative error of at most 0.0065.
Values may be sent and summed in bfloat16 or wider, within the bound.
A program may use at most 64 MiB of HBM per device.

v0:
```python
import jax
import jax.numpy as jnp
from jax import lax
from jax.sharding import PartitionSpec as P

HEAD_SIZE = 64


EPS = 1e-05


def softmax_probability(scores, sink_logit_bias):
    top = jnp.maximum(jnp.max(scores, axis=-1, keepdims=True), sink_logit_bias)
    expo = jnp.exp(scores - top)
    total = jnp.sum(expo, axis=-1, keepdims=True) + jnp.exp(sink_logit_bias - top)
    return (expo / total).astype(jnp.bfloat16)


def rms_norm(stream, gain):
    mean_sq = jnp.mean(stream * stream, axis=-1, keepdims=True)
    return (stream * lax.rsqrt(mean_sq + EPS) * gain).astype(jnp.bfloat16)


def on_device(
    x_pre,
    x_dec,
    prefill_query_rows,
    prefill_key_values,
    decode_query_rows,
    decode_key_values,
    cache,
    cache_len,
    sinks,
    o_weight,
    norm_gain,
    expert_ids,
    route_logits,
    w_gate_up,
    w_down,
):
    pre_rows, width = x_pre.shape
    dec_rows = x_dec.shape[0]
    kv_heads = prefill_key_values.shape[2] // HEAD_SIZE
    q_heads = sinks.shape[0]
    head_group = q_heads // kv_heads
    kv_max = cache.shape[2]
    scale = HEAD_SIZE ** (-0.5)
    sink_logit_bias = sinks.reshape(kv_heads, head_group)[None, :, :, None]
    keys_here = prefill_key_values[0].reshape(pre_rows, kv_heads, HEAD_SIZE)
    values_here = prefill_key_values[1].reshape(pre_rows, kv_heads, HEAD_SIZE)
    query_rows = prefill_query_rows.reshape(pre_rows, kv_heads, head_group, HEAD_SIZE)
    scores = (
        jnp.einsum("qhgd,khd->qhgk", query_rows, keys_here, preferred_element_type=jnp.float32)
        * scale
    )
    places = jnp.arange(pre_rows, dtype=jnp.int32)
    visible = places[None, :] <= places[:, None]
    scores = jnp.where(visible[:, None, None, :], scores, -jnp.inf)
    weight_matrix = softmax_probability(scores, sink_logit_bias)
    pre_out = jnp.einsum(
        "qhgk,khd->qhgd", weight_matrix, values_here, preferred_element_type=jnp.float32
    )
    pre_out = pre_out.astype(jnp.bfloat16).reshape(pre_rows, q_heads * HEAD_SIZE)
    dec_queries = decode_query_rows.reshape(dec_rows, kv_heads, head_group, HEAD_SIZE)
    cached_key_rows = cache[0].reshape(dec_rows, kv_max, kv_heads, HEAD_SIZE)
    cached_value_rows = cache[1].reshape(dec_rows, kv_max, kv_heads, HEAD_SIZE)
    own_key_rows = decode_key_values[0].reshape(dec_rows, kv_heads, HEAD_SIZE)
    own_value_rows = decode_key_values[1].reshape(dec_rows, kv_heads, HEAD_SIZE)
    past_positions = (
        jnp.einsum(
            "shgd,sjhd->shgj", dec_queries, cached_key_rows, preferred_element_type=jnp.float32
        )
        * scale
    )
    live = jnp.arange(kv_max, dtype=jnp.int32)[None, :] < cache_len[:, None]
    past_positions = jnp.where(live[:, None, None, :], past_positions, -jnp.inf)
    own_token = (
        jnp.einsum("shgd,shd->shg", dec_queries, own_key_rows, preferred_element_type=jnp.float32)[
            ..., None
        ]
        * scale
    )
    dec_weights = softmax_probability(
        jnp.concatenate([past_positions, own_token], axis=-1), sink_logit_bias
    )
    dec_out = jnp.einsum(
        "shgj,sjhd->shgd",
        dec_weights[..., :kv_max],
        cached_value_rows,
        preferred_element_type=jnp.float32,
    )
    dec_out = (
        dec_out
        + dec_weights[..., kv_max:].astype(jnp.float32)
        * own_value_rows.astype(jnp.float32)[:, :, None, :]
    )
    dec_out = dec_out.astype(jnp.bfloat16).reshape(dec_rows, q_heads * HEAD_SIZE)
    attn_rows = jnp.concatenate([pre_out, dec_out], axis=0)
    resid = jnp.concatenate([x_pre, x_dec], axis=0).astype(jnp.float32)
    half = attn_rows.shape[0] // 2
    mine = lax.axis_index("hp") * half
    head_part = jnp.dot(
        attn_rows,
        lax.all_gather(o_weight, "ep", axis=1, tiled=True),
        preferred_element_type=jnp.float32,
    )
    summed = lax.psum_scatter(head_part, "hp", scatter_dimension=0, tiled=True)
    stream = lax.dynamic_slice_in_dim(resid, mine, half, 0) + summed
    normed = lax.all_gather(rms_norm(stream, norm_gain), "hp", axis=0, tiled=True)
    tokens_here, topk = expert_ids.shape
    holders = lax.axis_size("ep")
    experts = holders // 2
    slot = min(
        tokens_here, 2 * ((3 * max(1, (tokens_here * topk + experts - 1) // experts) + 3) // 4)
    )
    plane = slot // 2
    flat_ids = expert_ids.reshape(-1)
    onehot = (flat_ids[:, None] == jnp.arange(experts, dtype=jnp.int32)[None, :]).astype(jnp.int32)
    rank = jnp.sum(jnp.cumsum(onehot, axis=0) * onehot, axis=1) - 1
    position = (flat_ids * slot + rank).reshape(tokens_here, topk)
    columns = jnp.arange(experts * slot, dtype=jnp.int32)[None, None, :] == position[:, :, None]
    picked_rows = jnp.any(columns, axis=1).T.astype(jnp.bfloat16)
    per_expert = (
        jnp.dot(picked_rows, normed, preferred_element_type=jnp.float32)
        .astype(jnp.bfloat16)
        .reshape(experts, slot, width)
    )
    send = jnp.repeat(per_expert, 2, axis=0)
    own_plane = lax.dynamic_slice_in_dim(send, lax.axis_index("hp") * plane, plane, 1)
    arrived_plane = lax.all_to_all(own_plane, "ep", split_axis=0, concat_axis=0, tiled=True)
    arrived = lax.all_gather(arrived_plane, "hp", axis=1, tiled=True)
    rows = arrived.reshape(-1, width)
    gate = jnp.dot(rows, w_gate_up[0, 0], preferred_element_type=jnp.float32)
    upper = jnp.dot(rows, w_gate_up[0, 1], preferred_element_type=jnp.float32)
    hidden = ((upper + 1.0) * gate * jax.nn.sigmoid(1.702 * gate)).astype(jnp.bfloat16)
    partial_out = jnp.dot(hidden, w_down[0], preferred_element_type=jnp.float32).reshape(
        -1, slot, width
    )
    share = lax.psum_scatter(
        partial_out.astype(jnp.bfloat16), "hp", scatter_dimension=1, tiled=True
    )
    returned = lax.all_to_all(share, "ep", split_axis=0, concat_axis=0, tiled=True)
    mix = jax.nn.softmax(route_logits, axis=-1)
    blend = jnp.sum(jnp.where(columns, mix[:, :, None], 0.0), axis=1).reshape(
        tokens_here, experts, slot
    )
    blend = jnp.repeat(blend, 2, axis=1)
    blend_plane = lax.dynamic_slice_in_dim(blend, lax.axis_index("hp") * plane, plane, 2).reshape(
        tokens_here, holders * plane
    )
    terms = jnp.dot(
        blend_plane,
        returned.reshape(-1, width).astype(jnp.float32),
        precision=lax.Precision.HIGHEST,
    )
    moe = lax.psum_scatter(
        terms.astype(jnp.bfloat16), "hp", scatter_dimension=0, tiled=True
    ).astype(jnp.float32)
    return (stream + moe).astype(jnp.bfloat16)


def solution(mesh):
    placed = (
        P(("groups", "ep"), None),
        P(("groups", "ep"), None),
        P(("groups", "ep"), "hp"),
        P(None, ("groups", "ep"), "hp"),
        P(("groups", "ep"), "hp"),
        P(None, ("groups", "ep"), "hp"),
        P(None, ("groups", "ep"), None, "hp"),
        P(("groups", "ep")),
        P("hp"),
        P("hp", "ep"),
        P(),
        P(("groups", "ep"), None),
        P(("groups", "ep"), None),
        P("ep", None, None, "hp"),
        P("ep", "hp", None),
    )
    return jax.shard_map(
        on_device,
        mesh=mesh,
        in_specs=placed,
        out_specs=P(("groups", "ep", "hp"), None),
        check_vma=False,
    )
```

profile of v0, /device:TPU:0, one launch (start us, length us, event | category | flops | bytes accessed | tf_op | source)
XLA Modules:
  0.0 216.3 jit_solution(10422376855241192798)
XLA Ops:
  6.6 0.7 all-gather.3.cloned.1.call-update
  7.3 0.8 copy.129
  8.3 1.1 fusion.34
  10.6 0.7 copy.123
  14.0 0.6 reduce-window.6
  14.6 66.1 %all-gather.3.cloned.1.call-done = bf16[1024,1536]{0,1:T(8,128)(2,1)} async-done(((bf16[1024,96]{0,1:T(8,128)(2,1)}), bf16[1024,1536]{0,1:T(8,128)(2,1)}) %all-gather.3.cloned.1.call-update) | async-done | bytes 3145744 | tf_op jit(solution)/shard_map/all_gather | solution.py:104
  80.8 3.7 %fusion.20 = f32[64,1536]{1,0:T(8,128)} fusion(bf16[1024,1536]{0,1:T(8,128)(2,1)} %all-gather.3.cloned.1.call-done, bf16[8,1024]{1,0:T(8,128)(2,1)S(1)} %reshape.149, bf16[56,1024]{1,0:T(8,128)(2,1)S(1)} %reshape.147), kind=kOutput, calls=%fused_computation.41 | convolution fusion | flops 201588736 | bytes 3670016 | tf_op jit(solution)/shard_map/dot_general | solution.py:102
  85.2 5.8 %reduce-scatter.6.cloned.1.call-done = f32[32,1536]{1,0:T(8,128)} async-done(((f32[64,1536]{1,0:T(8,128)}), f32[32,1536]{1,0:T(8,128)}) %reduce-scatter.6.cloned.1.call-update) | async-done | bytes 196624 | tf_op jit(solution)/shard_map/reduce_scatter | solution.py:107
  91.0 1.1 multiply_reduce_fusion
  92.2 1.9 all_gather.10
  95.0 37.1 %all_to_all.10 = bf16[16,24,1536]{2,1,0:T(8,128)(2,1)} all-to-all(bf16[16,24,1536]{2,1,0:T(8,128)(2,1)S(1)} %constant_dynamic-slice_fusion), channel_id=1, replica_groups=mesh['groups'=1,'ep'=16,'hp'=2] {'ep'}, dimensions={0} | all-to-all | bytes 2359296 | tf_op jit(solution)/shard_map/all_to_all | solution.py:130
  132.2 8.6 %all-gather.5.cloned.1.call-done = bf16[16,48,1536]{2,1,0:T(8,128)(2,1)} async-done(((bf16[16,24,1536]{2,1,0:T(8,128)(2,1)}), bf16[16,48,1536]{2,1,0:T(8,128)(2,1)}) %all-gather.5.cloned.1.call-update) | async-done | bytes 2359312 | tf_op jit(solution)/shard_map/all_gather | solution.py:131
  140.8 3.5 %fusion.7 = f32[768,384]{1,0:T(8,128)S(1)} fusion(bf16[768,1536]{1,0:T(8,128)(2,1)} %bitcast.84, bf16[1,2,1536,384]{3,2,1,0:T(8,128)(2,1)} %param.28), kind=kOutput, calls=%fused_computation.13 | convolution fusion | flops 905969664 | bytes 4718592 | tf_op jit(solution)/shard_map/dot_general | solution.py:133
  144.3 1.5 fusion.3
  145.8 1.4 fusion.38
  147.2 1.6 copy.149
  148.9 11.4 %reduce-scatter.10.cloned.1.call-done = bf16[24,24576]{1,0:T(8,128)(2,1)} async-done(((bf16[48,24576]{1,0:T(8,128)(2,1)}), bf16[24,24576]{1,0:T(8,128)(2,1)}) %reduce-scatter.10.cloned.1.call-update) | async-done | bytes 1179664
  160.3 1.6 copy.150
  161.9 1.7 copy.146
  163.6 7.0 %all-to-all-start.1 = ((bf16[16,24,1536]{2,1,0:T(8,128)(2,1)}), bf16[16,24,1536]{2,1,0:T(8,128)(2,1)S(1)}, u32[]{:S(2)}, u32[]{:S(2)}) async-start(bf16[16,24,1536]{2,1,0:T(8,128)(2,1)} %copy.146), calls=%async_computation.2 | async-start | bytes 2359296 | tf_op jit(solution)/shard_map/all_to_all | solution.py:142
  171.0 26.7 %all-to-all-done.1 = bf16[16,24,1536]{2,1,0:T(8,128)(2,1)S(1)} async-done(((bf16[16,24,1536]{2,1,0:T(8,128)(2,1)}), bf16[16,24,1536]{2,1,0:T(8,128)(2,1)S(1)}, u32[]{:S(2)}, u32[]{:S(2)}) %all-to-all-start.1) | async-done | bytes 1179680 | tf_op jit(solution)/shard_map/all_to_all | solution.py:142
  197.7 1.5 fusion
  199.2 9.0 %reduce-scatter.8.cloned.1.call-done = bf16[32,1536]{1,0:T(8,128)(2,1)} async-done(((bf16[64,1536]{1,0:T(8,128)(2,1)}), bf16[32,1536]{1,0:T(8,128)(2,1)}) %reduce-scatter.8.cloned.1.call-update) | async-done | bytes 98320 | tf_op jit(solution)/shard_map/reduce_scatter | solution.py:156
  208.2 1.6 add_convert_fusion
  (94 shorter events, 6.2 us)
Async XLA Ops:
  6.5 139.3 %copy-start = (bf16[1,384,1536]{2,1,0:T(8,128)(2,1)S(1)}, bf16[1,384,1536]{2,1,0:T(8,128)(2,1)}, u32[]{:S(2)}) copy-start(bf16[1,384,1536]{2,1,0:T(8,128)(2,1)} %param.29) | copy-start | bytes 3538948
  6.5 3.0 %copy-start.6 = (bf16[8,1024]{1,0:T(8,128)(2,1)S(1)}, bf16[8,1024]{1,0:T(8,128)(2,1)}, u32[]{:S(2)}) copy-start(bf16[8,1024]{1,0:T(8,128)(2,1)} %param.19) | copy-start | bytes 49156
  6.5 3.1 %copy-start.12 = (f32[16]{0:T(128)S(1)}, f32[16]{0:T(128)}, u32[]{:S(2)}) copy-start(f32[16]{0:T(128)} %param.23) | copy-start | bytes 196
  6.5 3.2 %copy-start.9 = (bf16[2,8,128]{2,1,0:T(8,128)(2,1)S(1)}, bf16[2,8,128]{2,1,0:T(8,128)(2,1)}, u32[]{:S(2)}) copy-start(bf16[2,8,128]{2,1,0:T(8,128)(2,1)} %param.20) | copy-start | bytes 12292
  6.5 3.3 %copy-start.13 = (s32[8]{0:T(128)S(1)}, s32[8]{0:T(128)}, u32[]{:S(2)}) copy-start(s32[8]{0:T(128)} %param.22) | copy-start | bytes 100
  6.5 74.2 %all-gather.3.cloned.1.call-start = ((), (), s32[]{:S(2)}) async-start(), calls=%async_computation.5 | async-start | bytes 3342336 | tf_op jit(solution)/shard_map/all_gather | solution.py:104
  7.3 83.7 %reduce-scatter.6.cloned.1.call-start = ((), (), s32[]{:S(2)}) async-start(), calls=%async_computation.6 | async-start | bytes 589824 | tf_op jit(solution)/shard_map/reduce_scatter | solution.py:107
  11.6 0.8 copy-start.3
  11.7 0.9 copy-start.2
  14.6 70.5 %copy-start.8 = (s32[64,4]{0,1:T(4,128)S(1)}, s32[64,4]{0,1:T(4,128)}, u32[]{:S(2)}) copy-start(s32[64,4]{0,1:T(4,128)} %param.26) | copy-start | bytes 3076
  14.6 76.4 %copy-start.1 = (bf16[56,1536]{1,0:T(8,128)(2,1)S(1)}, bf16[56,1536]{1,0:T(8,128)(2,1)}, u32[]{:S(2)}) copy-start(bf16[56,1536]{1,0:T(8,128)(2,1)} %param.15) | copy-start | bytes 516100
  14.6 76.4 %copy-start.4 = (bf16[8,1536]{1,0:T(8,128)(2,1)S(1)}, bf16[8,1536]{1,0:T(8,128)(2,1)}, u32[]{:S(2)}) copy-start(bf16[8,1536]{1,0:T(8,128)(2,1)} %param.16) | copy-start | bytes 73732
  14.6 77.5 %copy-start.7 = (f32[1536]{0:T(1024)S(1)}, f32[1536]{0:T(1024)}, u32[]{:S(2)}) copy-start(f32[1536]{0:T(1024)} %param.25) | copy-start | bytes 18436
  84.5 56.3 %all-gather.5.cloned.1.call-start = ((), (), s32[]{:S(2)}) async-start(), calls=%async_computation.7 | async-start | bytes 3538944 | tf_op jit(solution)/shard_map/all_gather | solution.py:131
  132.2 28.1 %reduce-scatter.10.cloned.1.call-start = ((), (), s32[]{:S(2)}) async-start(), calls=%async_computation.9 | async-start | bytes 3538944
  140.8 3.5 %copy-start.10 = (bf16[1,2,1536,384]{3,2,1,0:T(8,128)(2,1)S(1)}, bf16[1,2,1536,384]{3,2,1,0:T(8,128)(2,1)}, u32[]{:S(2)}) copy-start(bf16[1,2,1536,384]{3,2,1,0:T(8,128)(2,1)} %param.28) | copy-start | bytes 7077892
  140.8 3.5 %copy-start.11 = (bf16[16,48,1536]{2,1,0:T(8,128)(2,1)S(1)}, bf16[16,48,1536]{2,1,0:T(8,128)(2,1)}, u32[]{:S(2)}) copy-start(bf16[16,48,1536]{2,1,0:T(8,128)(2,1)} %all-gather.5.cloned.1.call-done) | copy-start | bytes 7077892
  163.6 7.1 %copy-start.5 = (f32[64,4]{0,1:T(4,128)S(1)}, f32[64,4]{0,1:T(4,128)}, u32[]{:S(2)}) copy-start(f32[64,4]{0,1:T(4,128)} %param.27) | copy-start | bytes 3076
  163.6 34.1 %all-to-all-start.1 = ((bf16[16,24,1536]{2,1,0:T(8,128)(2,1)}), bf16[16,24,1536]{2,1,0:T(8,128)(2,1)S(1)}, u32[]{:S(2)}, u32[]{:S(2)}) async-start(bf16[16,24,1536]{2,1,0:T(8,128)(2,1)} %copy.146), calls=%async_computation.2 | async-start | bytes 2359296 | tf_op jit(solution)/shard_map/all_to_all | solution.py:142
  170.6 37.6 %reduce-scatter.8.cloned.1.call-start = ((), (), s32[]{:S(2)}) async-start(), calls=%async_computation.8 | async-start | bytes 294912 | tf_op jit(solution)/shard_map/reduce_scatter | solution.py:156
Sparse Core Ops, SparseCore 0:
  10.1 70.5 all-gather.2
  84.6 6.3 reduce-scatter.5
  132.3 8.4 all-gather.4
  149.0 11.2 reduce-scatter.9
  199.3 8.8 reduce-scatter.7
where the time goes:
time: 217 us; the launch traced here: 216 us
  waiting for transfers between devices  128 us (59%)
  blocking collectives  39.1 us (18%)
  matrix products  13.5 us (6%)
  between operations  13.5 us (6%)
  local copies, waits for them, and re-layouts  10.1 us (5%)
  starting transfers between devices  7.24 us (3%)
  other arithmetic  4.54 us (2%)
    all_gather x1, waiting for transfers between devices, on_device(): lax.all_gather(o_weight, 'ep', axis=1, tiled=True)  66.1 us
    all_to_all x1, blocking collectives, on_device(): lax.all_to_all(own_plane, 'ep', split_axis=0, concat_axis=0, tiled=True)  37.1 us
    all_to_all x1, waiting for transfers between devices, on_device(): lax.all_to_all(share, 'ep', split_axis=0, concat_axis=0, tiled=True)  26.7 us
    unnamed x6, waiting for transfers between devices  12.2 us
    reduce_scatter x1, waiting for transfers between devices, on_device(): lax.psum_scatter(terms.astype(jnp.bfloat16), 'hp', scatter_dimension=0, t...  9.02 us
    all_gather x1, waiting for transfers between devices, on_device(): arrived = lax.all_gather(arrived_plane, 'hp', axis=1, tiled=True)  8.55 us
    all_to_all x1, starting transfers between devices, on_device(): lax.all_to_all(share, 'ep', split_axis=0, concat_axis=0, tiled=True)  7.04 us
    reduce_scatter x1, waiting for transfers between devices, on_device(): summed = lax.psum_scatter(head_part, 'hp', scatter_dimension=0, tiled=True)  5.76 us
  transfers between devices with their start and end apart: 6, of which 6 were waited for; matrix products, arithmetic and copies ran while one was open for 4% of the time, Pallas kernels for 0%

commit v1 on v0

--- a/solution.py
+++ b/solution.py
@@ -1,6 +1,10 @@
+import functools
+
 import jax
 import jax.numpy as jnp
 from jax import lax
+from jax.experimental import pallas as pl
+from jax.experimental.pallas import tpu as pltpu
 from jax.sharding import PartitionSpec as P
 
 HEAD_SIZE = 64
@@ -21,7 +25,76 @@
     return (stream * lax.rsqrt(mean_sq + EPS) * gain).astype(jnp.bfloat16)
 
 
-def on_device(
+def attention_rows(
+    x_pre,
+    x_dec,
+    prefill_query_rows,
+    prefill_key_values,
+    decode_query_rows,
+    decode_key_values,
+    cache,
+    cache_len,
+    sinks):
+    pre_rows, width = x_pre.shape
+    dec_rows = x_dec.shape[0]
+    kv_heads = prefill_key_values.shape[2] // HEAD_SIZE
+    q_heads = sinks.shape[0]
+    head_group = q_heads // kv_heads
+    kv_max = cache.shape[2]
+    scale = HEAD_SIZE ** (-0.5)
+    sink_logit_bias = sinks.reshape(kv_heads, head_group)[None, :, :, None]
+    keys_here = prefill_key_values[0].reshape(pre_rows, kv_heads, HEAD_SIZE)
+    values_here = prefill_key_values[1].reshape(pre_rows, kv_heads, HEAD_SIZE)
+    query_rows = prefill_query_rows.reshape(pre_rows, kv_heads, head_group, HEAD_SIZE)
+    scores = (
+        jnp.einsum("qhgd,khd->qhgk", query_rows, keys_here, preferred_element_type=jnp.float32)
+        * scale
+    )
+    places = jnp.arange(pre_rows, dtype=jnp.int32)
+    visible = places[None, :] <= places[:, None]
+    scores = jnp.where(visible[:, None, None, :], scores, -jnp.inf)
+    weight_matrix = softmax_probability(scores, sink_logit_bias)
+    pre_out = jnp.einsum(
+        "qhgk,khd->qhgd", weight_matrix, values_here, preferred_element_type=jnp.float32
+    )
+    pre_out = pre_out.astype(jnp.bfloat16).reshape(pre_rows, q_heads * HEAD_SIZE)
+    dec_queries = decode_query_rows.reshape(dec_rows, kv_heads, head_group, HEAD_SIZE)
+    cached_key_rows = cache[0].reshape(dec_rows, kv_max, kv_heads, HEAD_SIZE)
+    cached_value_rows = cache[1].reshape(dec_rows, kv_max, kv_heads, HEAD_SIZE)
+    own_key_rows = decode_key_values[0].reshape(dec_rows, kv_heads, HEAD_SIZE)
+    own_value_rows = decode_key_values[1].reshape(dec_rows, kv_heads, HEAD_SIZE)
+    past_positions = (
+        jnp.einsum(
+            "shgd,sjhd->shgj", dec_queries, cached_key_rows, preferred_element_type=jnp.float32
+        )
+        * scale
+    )
+    live = jnp.arange(kv_max, dtype=jnp.int32)[None, :] < cache_len[:, None]
+    past_positions = jnp.where(live[:, None, None, :], past_positions, -jnp.inf)
+    own_token = (
+        jnp.einsum("shgd,shd->shg", dec_queries, own_key_rows, preferred_element_type=jnp.float32)[
+            ..., None
+        ]
+        * scale
+    )
+    dec_weights = softmax_probability(
+        jnp.concatenate([past_positions, own_token], axis=-1), sink_logit_bias
+    )
+    dec_out = jnp.einsum(
+        "shgj,sjhd->shgd",
+        dec_weights[..., :kv_max],
+        cached_value_rows,
+        preferred_element_type=jnp.float32,
+    )
+    dec_out = (
+        dec_out
+        + dec_weights[..., kv_max:].astype(jnp.float32)
+        * own_value_rows.astype(jnp.float32)[:, :, None, :]
+    )
+    dec_out = dec_out.astype(jnp.bfloat16).reshape(dec_rows, q_heads * HEAD_SIZE)
+    attn_rows = jnp.concatenate([pre_out, dec_out], axis=0)
+    return attn_rows
+def general_path(
     x_pre,
     x_dec,
     prefill_query_rows,
@@ -38,64 +111,18 @@
     w_gate_up,
     w_down,
 ):
-    pre_rows, width = x_pre.shape
-    dec_rows = x_dec.shape[0]
-    kv_heads = prefill_key_values.shape[2] // HEAD_SIZE
-    q_heads = sinks.shape[0]
-    head_group = q_heads // kv_heads
-    kv_max = cache.shape[2]
-    scale = HEAD_SIZE ** (-0.5)
-    sink_logit_bias = sinks.reshape(kv_heads, head_group)[None, :, :, None]
-    keys_here = prefill_key_values[0].reshape(pre_rows, kv_heads, HEAD_SIZE)
-    values_here = prefill_key_values[1].reshape(pre_rows, kv_heads, HEAD_SIZE)
-    query_rows = prefill_query_rows.reshape(pre_rows, kv_heads, head_group, HEAD_SIZE)
-    scores = (
-        jnp.einsum("qhgd,khd->qhgk", query_rows, keys_here, preferred_element_type=jnp.float32)
-        * scale
-    )
-    places = jnp.arange(pre_rows, dtype=jnp.int32)
-    visible = places[None, :] <= places[:, None]
-    scores = jnp.where(visible[:, None, None, :], scores, -jnp.inf)
-    weight_matrix = softmax_probability(scores, sink_logit_bias)
-    pre_out = jnp.einsum(
-        "qhgk,khd->qhgd", weight_matrix, values_here, preferred_element_type=jnp.float32
-    )
-    pre_out = pre_out.astype(jnp.bfloat16).reshape(pre_rows, q_heads * HEAD_SIZE)
-    dec_queries = decode_query_rows.reshape(dec_rows, kv_heads, head_group, HEAD_SIZE)
-    cached_key_rows = cache[0].reshape(dec_rows, kv_max, kv_heads, HEAD_SIZE)
-    cached_value_rows = cache[1].reshape(dec_rows, kv_max, kv_heads, HEAD_SIZE)
-    own_key_rows = decode_key_values[0].reshape(dec_rows, kv_heads, HEAD_SIZE)
-    own_value_rows = decode_key_values[1].reshape(dec_rows, kv_heads, HEAD_SIZE)
-    past_positions = (
-        jnp.einsum(
-            "shgd,sjhd->shgj", dec_queries, cached_key_rows, preferred_element_type=jnp.float32
-        )
-        * scale
-    )
-    live = jnp.arange(kv_max, dtype=jnp.int32)[None, :] < cache_len[:, None]
-    past_positions = jnp.where(live[:, None, None, :], past_positions, -jnp.inf)
-    own_token = (
-        jnp.einsum("shgd,shd->shg", dec_queries, own_key_rows, preferred_element_type=jnp.float32)[
-            ..., None
-        ]
-        * scale
-    )
-    dec_weights = softmax_probability(
-        jnp.concatenate([past_positions, own_token], axis=-1), sink_logit_bias
-    )
-    dec_out = jnp.einsum(
-        "shgj,sjhd->shgd",
-        dec_weights[..., :kv_max],
-        cached_value_rows,
-        preferred_element_type=jnp.float32,
-    )
-    dec_out = (
-        dec_out
-        + dec_weights[..., kv_max:].astype(jnp.float32)
-        * own_value_rows.astype(jnp.float32)[:, :, None, :]
-    )
-    dec_out = dec_out.astype(jnp.bfloat16).reshape(dec_rows, q_heads * HEAD_SIZE)
-    attn_rows = jnp.concatenate([pre_out, dec_out], axis=0)
+    attn_rows = attention_rows(
+        x_pre,
+        x_dec,
+        prefill_query_rows,
+        prefill_key_values,
+        decode_query_rows,
+        decode_key_values,
+        cache,
+        cache_len,
+        sinks,
+    )
+    width = x_pre.shape[1]
     resid = jnp.concatenate([x_pre, x_dec], axis=0).astype(jnp.float32)
     half = attn_rows.shape[0] // 2
     mine = lax.axis_index("hp") * half
@@ -157,6 +184,329 @@
         terms.astype(jnp.bfloat16), "hp", scatter_dimension=0, tiled=True
     ).astype(jnp.float32)
     return (stream + moe).astype(jnp.bfloat16)
+
+
+MESH = pl.DeviceIdType.MESH
+SIDE = 2
+
+
+def layer_kernel(
+    depth_z,
+    attn_ref,
+    wo_ref,
+    x_ref,
+    gain_ref,
+    blend_ref,
+    gu_hbm,
+    dn_hbm,
+    out_ref,
+    wo_all,
+    mix_all,
+    mix_cols,
+    proj,
+    proj_in,
+    tok,
+    part_out,
+    from_core,
+    from_first,
+    mid,
+    from_z,
+    last_out,
+    from_last,
+    gu,
+    dn,
+    send_sem,
+    recv_sem,
+    load_sem,
+):
+    zs = depth_z
+    me = lax.axis_index("ep")
+    core = lax.axis_index("hp")
+    x, y, z = lax.rem(me, 2), lax.rem(me // 2, 2), me // 4
+    other = 1 - core
+    to_x = {"ep": z * 4 + y * 2 + (1 - x)}
+    to_y = {"ep": z * 4 + (1 - y) * 2 + x}
+    to_z = [None] + [{"ep": lax.rem(z + d, zs) * 4 + y * 2 + x} for d in range(1, zs)]
+    to_core = {"hp": other}
+
+    load_gu = pltpu.make_async_copy(gu_hbm, gu, load_sem.at[0])
+    load_dn = pltpu.make_async_copy(dn_hbm, dn, load_sem.at[1])
+    load_gu.start()
+    load_dn.start()
+
+    barrier = pltpu.get_barrier_semaphore()
+    partners = [to_x, to_y, to_core] + to_z[1:]
+    for partner in partners:
+        pl.semaphore_signal(barrier, inc=1, device_id=partner, device_id_type=MESH)
+    for p in range(2):
+        wo_all[p, z, y, x] = wo_ref[p]
+    mix_all[z, y, x] = blend_ref[...]
+    pl.semaphore_wait(barrier, len(partners))
+
+    sent = []
+
+    def push(source, target, device):
+        i = len(sent)
+        copy = pltpu.make_async_remote_copy(
+            src_ref=source,
+            dst_ref=target,
+            send_sem=send_sem.at[i],
+            recv_sem=recv_sem.at[i],
+            device_id=device,
+            device_id_type=MESH,
+        )
+        copy.start()
+        sent.append(copy)
+        return copy
+
+    def gather(lanes):
+        def near(first_y, zz, flip):
+            return (zz, 1 - y if flip else y, x) if first_y else (zz, y, 1 - x if flip else x)
+
+        first, second, across = [], [], []
+        for view, first_y in lanes:
+            own = view(z, y, x)
+            first.append(push(own, own, to_y if first_y else to_x))
+        for view, first_y in lanes:
+            own = view(z, y, x)
+            second.append([[push(own, own, to_z[d]) for d in range(1, zs)]])
+        for view, first_y in lanes:
+            own = view(z, y, x)
+            across.append([push(own, own, to_x if first_y else to_y)])
+        for n, (view, first_y) in enumerate(lanes):
+            first[n].wait_recv()
+            block = view(*near(first_y, z, True))
+            second[n].append([push(block, block, to_z[d]) for d in range(1, zs)])
+            across[n].append(push(block, block, to_x if first_y else to_y))
+        for flip in (False, True):
+            for d in range(1, zs):
+                for n, (view, first_y) in enumerate(lanes):
+                    second[n][int(flip)][d - 1].wait_recv()
+                    block = view(*near(first_y, lax.rem(z - d + zs, zs), flip))
+                    across[n].append(push(block, block, to_x if first_y else to_y))
+        return across
+
+    def settle(across):
+        for copies in across:
+            for copy in copies:
+                copy.wait_recv()
+
+    settle(
+        gather(
+            [
+                (lambda *at: wo_all.at[(0, *at)], True),
+                (lambda *at: wo_all.at[(1, *at)], False),
+                (lambda *at: mix_all.at[at], True),
+            ]
+        )
+    )
+
+    rows, inner = attn_ref.shape
+    half = rows // 2
+    split = inner // 2
+    width = x_ref.shape[1]
+    nt = (((1,), (1,)), ((), ()))
+    piece = width // zs
+    for j in range(zs):
+        total = 0.0
+        for p in range(2):
+            weight = wo_all[p, j].reshape(piece, split)
+            total = total + lax.dot_general(
+                attn_ref[:, p * split : (p + 1) * split],
+                weight,
+                nt,
+                preferred_element_type=jnp.float32,
+            )
+        proj[0, :, j * piece : (j + 1) * piece] = total[:half]
+        proj[1, :, j * piece : (j + 1) * piece] = total[half:]
+    exchange = push(proj.at[other], proj_in, to_core)
+
+    expert = me // 2
+    experts_rows = jnp.concatenate(
+        [
+            mix_all[a, b, c, pl.ds(expert, 1), :]
+            for a in range(zs)
+            for b in range(2)
+            for c in range(2)
+        ],
+        axis=0,
+    )
+    mix_cols[...] = experts_rows.T
+
+    exchange.wait_recv()
+    mine = pl.ds(pl.multiple_of(core * half, half), half)
+    stream = x_ref[mine, :].astype(jnp.float32) + (proj[core] + proj_in[...])
+    proj[core] = stream
+    mean_sq = jnp.mean(stream * stream, axis=-1, keepdims=True)
+    normed = (stream * lax.rsqrt(mean_sq + EPS) * gain_ref[...]).astype(jnp.bfloat16)
+    r = half // 2
+    for p in range(2):
+        tok[core, p, z, y, x] = normed[p * r : (p + 1) * r]
+    across = gather(
+        [
+            (lambda *at: tok.at[(core, 0, *at)], True),
+            (lambda *at: tok.at[(core, 1, *at)], False),
+        ]
+    )
+    whole = lambda p: tok.at[core, p]
+    near0 = tok.at[core, 0, :, :, x]
+    near1 = tok.at[core, 1, :, y]
+    over = [[push(near0, near0, to_core)], [push(near1, near1, to_core)]]
+    far0 = tok.at[core, 0, :, :, 1 - x]
+    far1 = tok.at[core, 1, :, 1 - y]
+    settle(across[:1])
+    over[0].append(push(far0, far0, to_core))
+    settle(across[1:])
+    over[1].append(push(far1, far1, to_core))
+    load_gu.wait()
+    load_dn.wait()
+
+    blocks = zs * 4
+
+    def expert_rows(side, p):
+        rows_in = tok[side, p].reshape(blocks * r, width)
+        gate = jnp.dot(rows_in, gu[0], preferred_element_type=jnp.float32)
+        upper = jnp.dot(rows_in, gu[1], preferred_element_type=jnp.float32)
+        cols = mix_cols[pl.ds(pl.multiple_of(side * half + p * r, r), r), :]
+        scale = jnp.concatenate([cols[:, b : b + 1] for b in range(blocks)], axis=0)
+        hidden = (upper + 1.0) * gate * jax.nn.sigmoid(1.702 * gate) * scale
+        result = jnp.dot(hidden.astype(jnp.bfloat16), dn[...], preferred_element_type=jnp.float32)
+        return result.reshape(zs, 2, 2, r, width)
+
+    back = []
+    for p in range(2):
+        for copy in over[p]:
+            copy.wait_recv()
+        part_out[other, p] = expert_rows(other, p).astype(jnp.bfloat16)
+        back.append(push(part_out.at[other, p], from_core.at[p], to_core))
+
+    firsts = []
+    for p in range(2):
+        result = expert_rows(core, p)
+        back[p].wait_recv()
+        part_out[core, p] = (result + from_core[p].astype(jnp.float32)).astype(jnp.bfloat16)
+        copies = []
+        for d in list(range(1, zs)) + [0]:
+            zt = lax.rem(z + d, zs)
+            if p == 0:
+                source, device = part_out.at[core, 0, zt, :, 1 - x], to_x
+            else:
+                source, device = part_out.at[core, 1, zt, 1 - y], to_y
+            copies.append(push(source, from_first.at[p, d], device))
+        firsts.append(copies)
+    order = list(range(1, zs)) + [0]
+    seconds = [[], []]
+    for k, d in enumerate(order):
+        for p in range(2):
+            zt = lax.rem(z + d, zs)
+            firsts[p][k].wait_recv()
+            kept = part_out[core, 0, zt, :, x] if p == 0 else part_out[core, 1, zt, y]
+            total = kept.astype(jnp.float32) + from_first[p, d].astype(jnp.float32)
+            mid[p, d] = total.astype(jnp.bfloat16)
+            if d:
+                seconds[p].append(push(mid.at[p, d], from_z.at[p, d - 1], to_z[d]))
+    lasts = []
+    for p in range(2):
+        total = mid[p, 0].astype(jnp.float32)
+        for d in range(1, zs):
+            seconds[p][d - 1].wait_recv()
+            total = total + from_z[p, d - 1].astype(jnp.float32)
+        last_out[p] = total
+        from_last[p, 0] = last_out[p, 1 - (y if p == 0 else x)].astype(jnp.bfloat16)
+        lasts.append(push(from_last.at[p, 0], from_last.at[p, 1], to_y if p == 0 else to_x))
+    for p in range(2):
+        lasts[p].wait_recv()
+        total = last_out[p, y if p == 0 else x] + from_last[p, 1].astype(jnp.float32)
+        out_ref[p * r : (p + 1) * r, :] = (proj[core, p * r : (p + 1) * r, :] + total).astype(
+            jnp.bfloat16
+        )
+    for copy in sent:
+        copy.wait_send()
+
+
+def fused_path(
+    holders,
+    x_pre,
+    x_dec,
+    prefill_query_rows,
+    prefill_key_values,
+    decode_query_rows,
+    decode_key_values,
+    cache,
+    cache_len,
+    sinks,
+    o_weight,
+    norm_gain,
+    expert_ids,
+    route_logits,
+    w_gate_up,
+    w_down,
+):
+    attn_rows = attention_rows(
+        x_pre,
+        x_dec,
+        prefill_query_rows,
+        prefill_key_values,
+        decode_query_rows,
+        decode_key_values,
+        cache,
+        cache_len,
+        sinks,
+    )
+    tokens, inner = attn_rows.shape
+    width = x_pre.shape[1]
+    hidden = w_down.shape[1]
+    columns = o_weight.shape[1]
+    zs = holders // 4
+    half, r = tokens // 2, tokens // 4
+    experts = holders // 2
+    resid = jnp.concatenate([x_pre, x_dec], axis=0)
+    wo = o_weight.reshape(2, inner // 2, columns).transpose(0, 2, 1)
+    mix = jax.nn.softmax(route_logits, axis=-1)
+    chosen = expert_ids[None, :, :] == jnp.arange(experts, dtype=jnp.int32)[:, None, None]
+    blend = jnp.sum(jnp.where(chosen, mix[None], 0.0), axis=-1)
+    blend = jnp.pad(blend, ((0, 0), (0, -tokens % 128)))
+    bf = jnp.bfloat16
+    grid = (zs, 2, 2)
+    return pl.pallas_call(
+        functools.partial(layer_kernel, zs),
+        out_shape=jax.ShapeDtypeStruct((half, width), bf),
+        in_specs=[pl.BlockSpec(memory_space=pltpu.VMEM)] * 5
+        + [pl.BlockSpec(memory_space=pl.ANY)] * 2,
+        out_specs=pl.BlockSpec(memory_space=pltpu.VMEM),
+        scratch_shapes=[
+            pltpu.VMEM((2, *grid, columns, inner // 2), bf),
+            pltpu.VMEM((*grid, *blend.shape), jnp.float32),
+            pltpu.VMEM((blend.shape[1], holders), jnp.float32),
+            pltpu.VMEM((2, half, width), jnp.float32),
+            pltpu.VMEM((half, width), jnp.float32),
+            pltpu.VMEM((2, 2, *grid, r, width), bf),
+            pltpu.VMEM((2, 2, *grid, r, width), bf),
+            pltpu.VMEM((2, *grid, r, width), bf),
+            pltpu.VMEM((2, zs, 2, r, width), bf),
+            pltpu.VMEM((2, zs, 2, r, width), bf),
+            pltpu.VMEM((2, zs - 1, 2, r, width), bf),
+            pltpu.VMEM((2, 2, r, width), jnp.float32),
+            pltpu.VMEM((2, 2, r, width), bf),
+            pltpu.VMEM((2, width, hidden), bf),
+            pltpu.VMEM((hidden, width), bf),
+            pltpu.SemaphoreType.DMA((192,)),
+            pltpu.SemaphoreType.DMA((192,)),
+            pltpu.SemaphoreType.DMA((2,)),
+        ],
+        compiler_params=pltpu.CompilerParams(
+            collective_id=0, has_side_effects=True, vmem_limit_bytes=60 * 2**20
+        ),
+    )(attn_rows, wo, resid, norm_gain.reshape(1, width), blend, w_gate_up[0], w_down[0])
+
+
+def on_device(holders, *args):
+    x_pre, x_dec, o_weight = args[0], args[1], args[9]
+    tokens = x_pre.shape[0] + x_dec.shape[0]
+    gathered = 2 * holders * (tokens * x_pre.shape[1] * 4 + o_weight.size)
+    if holders % 4 == 0 and holders >= 8 and tokens % 64 == 0 and gathered < 32 * 2**20:
+        return fused_path(holders, *args)
+    return general_path(*args)
 
 
 def solution(mesh):
@@ -178,7 +528,7 @@
         P("ep", "hp", None),
     )
     return jax.shard_map(
-        on_device,
+        functools.partial(on_device, mesh.shape["ep"]),
         mesh=mesh,
         in_specs=placed,
         out_specs=P(("groups", "ep", "hp"), None),

time: 217 us -> 116 us (0.53)
  waiting for transfers between devices: 128 us -> 0 us
  Pallas kernels: 0 us -> 103 us
  blocking collectives: 39.1 us -> 0 us
  between operations: 13.5 us -> 0.27 us
  matrix products: 13.5 us -> 1.34 us
  starting transfers between devices: 7.24 us -> 0 us
  local copies, waits for them, and re-layouts: 10.1 us -> 7.16 us
  other arithmetic: 4.54 us -> 2.16 us
    pallas_call x0 -> x1, Pallas kernels: none -> 103 us  [fused_path(): pl.pallas_call(functools.partial(layer_kernel, zs), out_shape=jax.ShapeDt...]
    all_gather x2 -> x0, waiting for transfers between devices: 74.7 us -> none  [the longest x1 66.1 us: on_device(): lax.all_gather(o_weight, 'ep', axis=1, tiled=True)]
    all_to_all x1 -> x0, blocking collectives: 37.1 us -> none  [on_device(): lax.all_to_all(own_plane, 'ep', split_axis=0, concat_axis=0, tiled=True)]
    all_to_all x1 -> x0, waiting for transfers between devices: 26.7 us -> none  [on_device(): lax.all_to_all(share, 'ep', split_axis=0, concat_axis=0, tiled=True)]
    reduce_scatter x2 -> x0, waiting for transfers between devices: 14.8 us -> none  [the longest x1 9.02 us: on_device(): lax.psum_scatter(terms.astype(jnp.bfloat16), 'hp', scatter_dimension=0, t...]
    unnamed x6 -> x0, waiting for transfers between devices: 12.2 us -> none
    dot_general x11 -> x5, matrix products: 13.5 us -> 1.34 us  [the longest x1 0.37 us: attention_rows(): jnp.einsum('qhgd,khd->qhgk', query_rows, keys_here, preferred_element_typ...]
    all_to_all x1 -> x0, starting transfers between devices: 7.04 us -> none  [on_device(): lax.all_to_all(share, 'ep', split_axis=0, concat_axis=0, tiled=True)]
  transfers between devices with their start and end apart: 6 -> 0, of which waited for: 6 -> 0; matrix products, arithmetic and copies ran while one was open for 4% -> 0% of each run, Pallas kernels for 0% -> 0%
where the time goes in v1:
time: 116 us; the launch traced here: 114 us
  Pallas kernels  103 us (89%)
  local copies, waits for them, and re-layouts  7.16 us (6%)
  other arithmetic  2.16 us (2%)
  matrix products  1.34 us (1%)
    pallas_call x1, Pallas kernels, fused_path(): pl.pallas_call(functools.partial(layer_kernel, zs), out_shape=jax.ShapeDt...  103 us

profile of v1, /device:TPU:0, one launch (start us, length us, event | category | flops | bytes accessed | tf_op | source)
XLA Modules:
  0.0 113.9 jit_solution(17970828754757213953)
XLA Ops:
  0.0 1.1 fusion.13
  1.1 0.2 copy.98
  1.4 0.2 copy.90
  1.7 0.3 fusion.15
  2.0 0.1 fusion.17
  2.3 0.2 copy.92
  2.5 0.7 copy.95
  3.2 0.1 exponential_reduce_fusion
  3.4 0.1 divide_convert_fusion
  3.7 0.3 fusion.4
  4.0 0.1 reshape.101
  4.1 0.3 copy-done.2
  4.5 0.2 reshape.98
  4.8 0.4 fusion.16
  5.2 0.1 fusion.6
  5.5 0.3 fusion.2
  5.9 0.2 reshape.99
  6.1 0.7 pad_maximum_fusion.1.attn_ref
  6.7 0.7 copy.130
  7.4 0.7 pad_maximum_fusion.x_ref
  8.1 0.6 reshape.103.gain_ref
  8.8 0.6 pad.4.blend_ref
  9.4 102.9 %shard_map.145 = bf16[32,1536]{1,0:T(8,128)(2,1)} custom-call(bf16[64,1024]{1,0:T(8,128)(2,1)} %pad_maximum_fusion.1.attn_ref, bf16[2,96,512]{2,1,0:T(8,128)(2,1)} %bitcast.40, bf16[64,1536]{1,0:T(8,128)(2,1)} %pad_maximum_fusion.x_ref, f32[1,1536]{1,0:T(1,128)} %reshape.103.gain_ref, f32[8,128]{1,0:T(8,128)} %pad.4.blend_ref, ...), custom_call_target="tpu_custom_call" | custom-call | tf_op jit(solution)/shard_map/pallas_call | solution.py:471
  112.3 1.5 %copy.132 = bf16[32,1536]{1,0:T(8,128)(2,1)} copy(bf16[32,1536]{1,0:T(8,128)(2,1)} %shard_map.145) | data formatting | bytes 196608
  (47 shorter events, 1.1 us)
Async XLA Ops:
  0.0 1.3 %copy-start.6 = (bf16[8,1024]{1,0:T(8,128)(2,1)S(1)}, bf16[8,1024]{1,0:T(8,128)(2,1)}, u32[]{:S(2)}) copy-start(bf16[8,1024]{1,0:T(8,128)(2,1)} %param.19) | copy-start | bytes 49156
  0.0 1.6 %copy-start.10 = (s32[8]{0:T(128)S(1)}, s32[8]{0:T(128)}, u32[]{:S(2)}) copy-start(s32[8]{0:T(128)} %param.22) | copy-start | bytes 100
  0.0 2.0 %copy-start.8 = (bf16[2,8,128]{2,1,0:T(8,128)(2,1)S(1)}, bf16[2,8,128]{2,1,0:T(8,128)(2,1)}, u32[]{:S(2)}) copy-start(bf16[2,8,128]{2,1,0:T(8,128)(2,1)} %param.20) | copy-start | bytes 12292
  0.0 2.2 %copy-start.11 = (f32[16]{0:T(128)S(1)}, f32[16]{0:T(128)}, u32[]{:S(2)}) copy-start(f32[16]{0:T(128)} %param.23) | copy-start | bytes 196
  3.6 0.9 copy-start.2
  3.6 1.1 copy-start.3
  5.5 1.2 %copy-start = (bf16[1024,96]{0,1:T(8,128)(2,1)S(1)}, bf16[1024,96]{0,1:T(8,128)(2,1)}, u32[]{:S(2)}) copy-start(bf16[1024,96]{0,1:T(8,128)(2,1)} %param.24) | copy-start | bytes 589828
  5.8 1.6 %copy-start.1 = (bf16[56,1536]{1,0:T(8,128)(2,1)S(1)}, bf16[56,1536]{1,0:T(8,128)(2,1)}, u32[]{:S(2)}) copy-start(bf16[56,1536]{1,0:T(8,128)(2,1)} %param.15) | copy-start | bytes 516100
  5.8 1.6 %copy-start.4 = (bf16[8,1536]{1,0:T(8,128)(2,1)S(1)}, bf16[8,1536]{1,0:T(8,128)(2,1)}, u32[]{:S(2)}) copy-start(bf16[8,1536]{1,0:T(8,128)(2,1)} %param.16) | copy-start | bytes 73732
  5.8 2.3 %copy-start.7 = (f32[1536]{0:T(1024)S(1)}, f32[1536]{0:T(1024)}, u32[]{:S(2)}) copy-start(f32[1536]{0:T(1024)} %param.25) | copy-start | bytes 18436
  5.8 2.9 %copy-start.5 = (f32[64,4]{0,1:T(4,128)S(1)}, f32[64,4]{0,1:T(4,128)}, u32[]{:S(2)}) copy-start(f32[64,4]{0,1:T(4,128)} %param.27) | copy-start | bytes 3076
  5.8 2.9 %copy-start.9 = (s32[64,4]{0,1:T(4,128)S(1)}, s32[64,4]{0,1:T(4,128)}, u32[]{:S(2)}) copy-start(s32[64,4]{0,1:T(4,128)} %param.26) | copy-start | bytes 3076

commit v2 on v1

--- a/solution.py
+++ b/solution.py
@@ -203,16 +203,19 @@
     wo_all,
     mix_all,
     mix_cols,
+    attn_all,
     proj,
     proj_in,
+    columns,
+    kept_rows,
     tok,
     part_out,
     from_core,
     from_first,
     mid,
+    from_second,
+    to_send,
     from_z,
-    last_out,
-    from_last,
     gu,
     dn,
     send_sem,
@@ -239,7 +242,7 @@
     for partner in partners:
         pl.semaphore_signal(barrier, inc=1, device_id=partner, device_id_type=MESH)
     for p in range(2):
-        wo_all[p, z, y, x] = wo_ref[p]
+        wo_all[p, y, x] = wo_ref[p]
     mix_all[z, y, x] = blend_ref[...]
     pl.semaphore_wait(barrier, len(partners))
 
@@ -260,66 +263,86 @@
         return copy
 
     def gather(lanes):
-        def near(first_y, zz, flip):
-            return (zz, 1 - y if flip else y, x) if first_y else (zz, y, 1 - x if flip else x)
-
-        first, second, across = [], [], []
-        for view, first_y in lanes:
+        along, second, last = [], [], []
+        for view, x_next in lanes:
             own = view(z, y, x)
-            first.append(push(own, own, to_y if first_y else to_x))
-        for view, first_y in lanes:
-            own = view(z, y, x)
-            second.append([[push(own, own, to_z[d]) for d in range(1, zs)]])
-        for view, first_y in lanes:
-            own = view(z, y, x)
-            across.append([push(own, own, to_x if first_y else to_y)])
-        for n, (view, first_y) in enumerate(lanes):
-            first[n].wait_recv()
-            block = view(*near(first_y, z, True))
-            second[n].append([push(block, block, to_z[d]) for d in range(1, zs)])
-            across[n].append(push(block, block, to_x if first_y else to_y))
-        for flip in (False, True):
-            for d in range(1, zs):
-                for n, (view, first_y) in enumerate(lanes):
-                    second[n][int(flip)][d - 1].wait_recv()
-                    block = view(*near(first_y, lax.rem(z - d + zs, zs), flip))
-                    across[n].append(push(block, block, to_x if first_y else to_y))
-        return across
+            along.append([push(own, own, to_z[d]) for d in range(1, zs)])
+            second.append([push(own, own, to_x if x_next else to_y)])
+            last.append([push(own, own, to_y if x_next else to_x)])
+        for d in range(zs):
+            zt = lax.rem(z - d + zs, zs)
+            for n, (view, x_next) in enumerate(lanes):
+                if d:
+                    along[n][d - 1].wait_recv()
+                    block = view(zt, y, x)
+                    second[n].append(push(block, block, to_x if x_next else to_y))
+                    last[n].append(push(block, block, to_y if x_next else to_x))
+        for d in range(zs):
+            zt = lax.rem(z - d + zs, zs)
+            for n, (view, x_next) in enumerate(lanes):
+                second[n][d].wait_recv()
+                block = view(zt, y, 1 - x) if x_next else view(zt, 1 - y, x)
+                last[n].append(push(block, block, to_y if x_next else to_x))
+        return last
 
     def settle(across):
         for copies in across:
             for copy in copies:
                 copy.wait_recv()
 
-    settle(
-        gather(
-            [
-                (lambda *at: wo_all.at[(0, *at)], True),
-                (lambda *at: wo_all.at[(1, *at)], False),
-                (lambda *at: mix_all.at[at], True),
-            ]
-        )
-    )
-
     rows, inner = attn_ref.shape
     half = rows // 2
     split = inner // 2
     width = x_ref.shape[1]
+    piece = width // zs
     nt = (((1,), (1,)), ((), ()))
-    piece = width // zs
-    for j in range(zs):
+
+    heads = [push(attn_ref, attn_all.at[d - 1], to_z[d]) for d in range(1, zs)]
+    own0, own1 = wo_all.at[0, y, x], wo_all.at[1, y, x]
+    weights = [push(own0, own0, to_y), push(own1, own1, to_x)]
+    weights += [push(own0, own0, to_x), push(own1, own1, to_y)]
+    own = mix_all.at[z, y, x]
+    mixes = [push(own, own, to_z[d]) for d in range(1, zs)]
+    weights[0].wait_recv()
+    near = wo_all.at[0, 1 - y, x]
+    weights.append(push(near, near, to_x))
+    weights[1].wait_recv()
+    near = wo_all.at[1, y, 1 - x]
+    weights.append(push(near, near, to_y))
+    for copy in mixes:
+        copy.wait_recv()
+    near = mix_all.at[:, y, x]
+    copy = push(near, near, to_y)
+    copy.wait_recv()
+    near = mix_all.at[:, :, x]
+    mixes = push(near, near, to_x)
+    for copy in weights[2:]:
+        copy.wait_recv()
+    exchange = []
+    for d in range(zs):
+        if d:
+            heads[d - 1].wait_recv()
+        queries = attn_all[d - 1] if d else attn_ref[...]
         total = 0.0
         for p in range(2):
-            weight = wo_all[p, j].reshape(piece, split)
             total = total + lax.dot_general(
-                attn_ref[:, p * split : (p + 1) * split],
-                weight,
+                queries[:, p * split : (p + 1) * split],
+                wo_all[p].reshape(piece, split),
                 nt,
                 preferred_element_type=jnp.float32,
             )
-        proj[0, :, j * piece : (j + 1) * piece] = total[:half]
-        proj[1, :, j * piece : (j + 1) * piece] = total[half:]
-    exchange = push(proj.at[other], proj_in, to_core)
+        proj[d, 0] = total[:half]
+        proj[d, 1] = total[half:]
+        exchange.append(push(proj.at[d, other], proj_in.at[d], to_core))
+    returns = []
+    for d in list(range(1, zs)) + [0]:
+        exchange[d].wait_recv()
+        if d:
+            proj[d, core] = proj[d, core] + proj_in[d]
+            returns.append(push(proj.at[d, core], columns.at[z], to_z[zs - d]))
+        else:
+            columns[z] = proj[0, core] + proj_in[0]
+    mixes.wait_recv()
 
     expert = me // 2
     experts_rows = jnp.concatenate(
@@ -333,10 +356,12 @@
     )
     mix_cols[...] = experts_rows.T
 
-    exchange.wait_recv()
+    for copy in returns:
+        copy.wait_recv()
     mine = pl.ds(pl.multiple_of(core * half, half), half)
-    stream = x_ref[mine, :].astype(jnp.float32) + (proj[core] + proj_in[...])
-    proj[core] = stream
+    added = jnp.concatenate([columns[a] for a in range(zs)], axis=1)
+    stream = x_ref[mine, :].astype(jnp.float32) + added
+    kept_rows[...] = stream
     mean_sq = jnp.mean(stream * stream, axis=-1, keepdims=True)
     normed = (stream * lax.rsqrt(mean_sq + EPS) * gain_ref[...]).astype(jnp.bfloat16)
     r = half // 2
@@ -348,76 +373,139 @@
             (lambda *at: tok.at[(core, 1, *at)], False),
         ]
     )
-    whole = lambda p: tok.at[core, p]
-    near0 = tok.at[core, 0, :, :, x]
-    near1 = tok.at[core, 1, :, y]
-    over = [[push(near0, near0, to_core)], [push(near1, near1, to_core)]]
-    far0 = tok.at[core, 0, :, :, 1 - x]
-    far1 = tok.at[core, 1, :, 1 - y]
-    settle(across[:1])
-    over[0].append(push(far0, far0, to_core))
-    settle(across[1:])
-    over[1].append(push(far1, far1, to_core))
+    def near(ref, side, p):
+        return ref.at[side, 0, :, y] if p == 0 else ref.at[side, 1, :, :, x]
+
+    def far(ref, side, p, zt):
+        return ref.at[side, 0, zt, 1 - y] if p == 0 else ref.at[side, 1, zt, :, 1 - x]
+
+    def expert_rows(rows_in, scale):
+        gate = jnp.dot(rows_in, gu[0], preferred_element_type=jnp.float32)
+        upper = jnp.dot(rows_in, gu[1], preferred_element_type=jnp.float32)
+        hidden = (upper + 1.0) * gate * jax.nn.sigmoid(1.702 * gate) * scale
+        result = jnp.dot(hidden.astype(jnp.bfloat16), dn[...], preferred_element_type=jnp.float32)
+        return result.astype(jnp.bfloat16)
+
+    def scales(side, p, places):
+        cols = mix_cols[pl.ds(pl.multiple_of(side * half + p * r, r), r), :]
+        lane = lax.broadcasted_iota(jnp.int32, cols.shape, 1)
+        return [
+            jnp.sum(jnp.where(lane == place, cols, 0.0), axis=1, keepdims=True) for place in places
+        ]
+
+    def place(zt, yy, xx):
+        return zt * 4 + yy * 2 + xx
+
+    over_near = [push(near(tok, core, p), near(tok, core, p), to_core) for p in range(2)]
     load_gu.wait()
     load_dn.wait()
 
-    blocks = zs * 4
-
-    def expert_rows(side, p):
-        rows_in = tok[side, p].reshape(blocks * r, width)
-        gate = jnp.dot(rows_in, gu[0], preferred_element_type=jnp.float32)
-        upper = jnp.dot(rows_in, gu[1], preferred_element_type=jnp.float32)
-        cols = mix_cols[pl.ds(pl.multiple_of(side * half + p * r, r), r), :]
-        scale = jnp.concatenate([cols[:, b : b + 1] for b in range(blocks)], axis=0)
-        hidden = (upper + 1.0) * gate * jax.nn.sigmoid(1.702 * gate) * scale
-        result = jnp.dot(hidden.astype(jnp.bfloat16), dn[...], preferred_element_type=jnp.float32)
-        return result.reshape(zs, 2, 2, r, width)
-
-    back = []
+    def run_near(side):
+        rows_in, scale = [], []
+        for p in range(2):
+            rows_in.append(near(tok, side, p)[...].reshape(2 * zs * r, width))
+            scale += scales(
+                side,
+                p,
+                [
+                    place(a, y, b) if p == 0 else place(a, b, x)
+                    for a in range(zs)
+                    for b in range(2)
+                ],
+            )
+        result = expert_rows(jnp.concatenate(rows_in, axis=0), jnp.concatenate(scale, axis=0))
+        result = result.reshape(2, zs, 2, r, width)
+        for p in range(2):
+            near(part_out, side, p)[...] = result[p]
+
+    def arrive(d):
+        zt = lax.rem(z - d + zs, zs)
+        copies = []
+        for p in range(2):
+            across[p][d].wait_recv()
+            across[p][zs + d].wait_recv()
+            copies.append(push(far(tok, core, p, zt), far(tok, core, p, zt), to_core))
+        return copies
+
+    def run_far(d, copies):
+        zt = lax.rem(z - d + zs, zs)
+        for copy in copies:
+            copy.wait_recv()
+        rows_in, scale = [], []
+        for side in (core, other):
+            for p in range(2):
+                rows_in.append(far(tok, side, p, zt)[...].reshape(2 * r, width))
+                scale += scales(
+                    side,
+                    p,
+                    [place(zt, 1 - y, b) if p == 0 else place(zt, b, 1 - x) for b in range(2)],
+                )
+        result = expert_rows(jnp.concatenate(rows_in, axis=0), jnp.concatenate(scale, axis=0))
+        result = result.reshape(2, 2, 2, r, width)
+        for n, side in enumerate((core, other)):
+            for p in range(2):
+                far(part_out, side, p, zt)[...] = result[n, p]
+        return [
+            push(far(part_out, other, p, zt), from_core.at[p, zs + d], to_core) for p in range(2)
+        ]
+
+    def add_far(d, copies):
+        zt = lax.rem(z - d + zs, zs)
+        started = []
+        for p in range(2):
+            copies[p].wait_recv()
+            block = far(part_out, core, p, zt)
+            total = block[...].astype(jnp.float32) + from_core[p, zs + d].astype(jnp.float32)
+            block[...] = total.astype(jnp.bfloat16)
+            started.append(push(block, from_first.at[p, d], to_y if p == 0 else to_x))
+        return started
+
+    run_near(core)
+    crossed = [arrive(0)]
+    for copy in over_near:
+        copy.wait_recv()
+    run_near(other)
+    near_back = [
+        push(near(part_out, other, p), from_core.at[p, pl.ds(0, zs)], to_core) for p in range(2)
+    ]
+    done, firsts = [], []
+    for d in range(zs):
+        if d + 1 < zs:
+            crossed.append(arrive(d + 1))
+        done.append(run_far(d, crossed[d]))
+        if d:
+            firsts.append(add_far(d - 1, done[d - 1]))
+    firsts.append(add_far(zs - 1, done[zs - 1]))
     for p in range(2):
-        for copy in over[p]:
-            copy.wait_recv()
-        part_out[other, p] = expert_rows(other, p).astype(jnp.bfloat16)
-        back.append(push(part_out.at[other, p], from_core.at[p], to_core))
-
-    firsts = []
+        near_back[p].wait_recv()
+    seconds, lasts = [[], []], [[], []]
+    for d in range(zs):
+        for p in range(2):
+            zt = lax.rem(z - d + zs, zs)
+            firsts[d][p].wait_recv()
+            kept = part_out[core, 0, zt, y] if p == 0 else part_out[core, 1, zt, :, x]
+            total = kept.astype(jnp.float32) + from_core[p, zt].astype(jnp.float32)
+            total = total + from_first[p, d].astype(jnp.float32)
+            mid[p, d] = total.astype(jnp.bfloat16)
+            away = mid.at[p, d, 1 - (x if p == 0 else y)]
+            seconds[p].append(push(away, from_second.at[p, d], to_x if p == 0 else to_y))
+    totals = []
+    for d in range(zs):
+        for p in range(2):
+            seconds[p][d].wait_recv()
+            kept = mid[p, d, x if p == 0 else y].astype(jnp.float32)
+            total = kept + from_second[p, d].astype(jnp.float32)
+            if d:
+                to_send[p, d - 1] = total.astype(jnp.bfloat16)
+                lasts[p].append(push(to_send.at[p, d - 1], from_z.at[p, d - 1], to_z[zs - d]))
+            else:
+                totals.append(total)
     for p in range(2):
-        result = expert_rows(core, p)
-        back[p].wait_recv()
-        part_out[core, p] = (result + from_core[p].astype(jnp.float32)).astype(jnp.bfloat16)
-        copies = []
-        for d in list(range(1, zs)) + [0]:
-            zt = lax.rem(z + d, zs)
-            if p == 0:
-                source, device = part_out.at[core, 0, zt, :, 1 - x], to_x
-            else:
-                source, device = part_out.at[core, 1, zt, 1 - y], to_y
-            copies.append(push(source, from_first.at[p, d], device))
-        firsts.append(copies)
-    order = list(range(1, zs)) + [0]
-    seconds = [[], []]
-    for k, d in enumerate(order):
-        for p in range(2):
-            zt = lax.rem(z + d, zs)
-            firsts[p][k].wait_recv()
-            kept = part_out[core, 0, zt, :, x] if p == 0 else part_out[core, 1, zt, y]
-            total = kept.astype(jnp.float32) + from_first[p, d].astype(jnp.float32)
-            mid[p, d] = total.astype(jnp.bfloat16)
-            if d:
-                seconds[p].append(push(mid.at[p, d], from_z.at[p, d - 1], to_z[d]))
-    lasts = []
-    for p in range(2):
-        total = mid[p, 0].astype(jnp.float32)
-        for d in range(1, zs):
-            seconds[p][d - 1].wait_recv()
-            total = total + from_z[p, d - 1].astype(jnp.float32)
-        last_out[p] = total
-        from_last[p, 0] = last_out[p, 1 - (y if p == 0 else x)].astype(jnp.bfloat16)
-        lasts.append(push(from_last.at[p, 0], from_last.at[p, 1], to_y if p == 0 else to_x))
-    for p in range(2):
-        lasts[p].wait_recv()
-        total = last_out[p, y if p == 0 else x] + from_last[p, 1].astype(jnp.float32)
-        out_ref[p * r : (p + 1) * r, :] = (proj[core, p * r : (p + 1) * r, :] + total).astype(
+        total = totals[p]
+        for e in range(1, zs):
+            lasts[p][e - 1].wait_recv()
+            total = total + from_z[p, e - 1].astype(jnp.float32)
+        out_ref[p * r : (p + 1) * r, :] = (kept_rows[p * r : (p + 1) * r, :] + total).astype(
             jnp.bfloat16
         )
     for copy in sent:
@@ -475,19 +563,22 @@
         + [pl.BlockSpec(memory_space=pl.ANY)] * 2,
         out_specs=pl.BlockSpec(memory_space=pltpu.VMEM),
         scratch_shapes=[
-            pltpu.VMEM((2, *grid, columns, inner // 2), bf),
+            pltpu.VMEM((2, 2, 2, columns, inner // 2), bf),
             pltpu.VMEM((*grid, *blend.shape), jnp.float32),
             pltpu.VMEM((blend.shape[1], holders), jnp.float32),
-            pltpu.VMEM((2, half, width), jnp.float32),
+            pltpu.VMEM((zs - 1, tokens, inner), bf),
+            pltpu.VMEM((zs, 2, half, width // zs), jnp.float32),
+            pltpu.VMEM((zs, half, width // zs), jnp.float32),
+            pltpu.VMEM((zs, half, width // zs), jnp.float32),
             pltpu.VMEM((half, width), jnp.float32),
             pltpu.VMEM((2, 2, *grid, r, width), bf),
             pltpu.VMEM((2, 2, *grid, r, width), bf),
-            pltpu.VMEM((2, *grid, r, width), bf),
+            pltpu.VMEM((2, 2 * zs, 2, r, width), bf),
             pltpu.VMEM((2, zs, 2, r, width), bf),
             pltpu.VMEM((2, zs, 2, r, width), bf),
-            pltpu.VMEM((2, zs - 1, 2, r, width), bf),
-            pltpu.VMEM((2, 2, r, width), jnp.float32),
-            pltpu.VMEM((2, 2, r, width), bf),
+            pltpu.VMEM((2, zs, r, width), bf),
+            pltpu.VMEM((2, zs - 1, r, width), bf),
+            pltpu.VMEM((2, zs - 1, r, width), bf),
             pltpu.VMEM((2, width, hidden), bf),
             pltpu.VMEM((hidden, width), bf),
             pltpu.SemaphoreType.DMA((192,)),

time: 116 us -> 89.7 us (0.77); the launches traced: 114 us -> 89.5 us
  Pallas kernels: 103 us -> 78.6 us
    pallas_call x1, Pallas kernels: 103 us -> 78.6 us  [fused_path(): pl.pallas_call(functools.partial(layer_kernel, zs), out_shape=jax.ShapeDt...]
where the time goes in v2:
time: 89.7 us; the launch traced here: 89.5 us
  Pallas kernels  78.6 us (88%)
  local copies, waits for them, and re-layouts  7.16 us (8%)
  other arithmetic  2.16 us (2%)
  matrix products  1.34 us (1%)
    pallas_call x1, Pallas kernels, fused_path(): pl.pallas_call(functools.partial(layer_kernel, zs), out_shape=jax.ShapeDt...  78.6 us
    unnamed x25, local copies, waits for them, and re-layouts  1.93 us

profile of v2, /device:TPU:0, one launch (start us, length us, event | category | flops | bytes accessed | tf_op | source)
XLA Modules:
  0.0 89.5 jit_solution(14233409240938786467)
XLA Ops:
  0.0 1.1 %fusion.13 = (bf16[1,8,128,128]{3,2,1,0:T(8,128)(2,1)S(1)}, bf16[1,8,128,128]{3,2,1,0:T(8,128)(2,1)S(1)}) fusion(bf16[2,8,128,128]{3,2,1,0:T(8,128)(2,1)} %param.21), kind=kLoop, calls=%fused_computation.37 | loop fusion | bytes 1048576 | tf_op jit(solution)/shard_map/slice | solution.py:62
  1.1 0.2 copy.98
  1.4 0.2 copy.90
  1.7 0.3 fusion.15
  2.0 0.1 fusion.17
  2.3 0.2 copy.92
  2.5 0.7 copy.95
  3.2 0.1 exponential_reduce_fusion
  3.4 0.1 divide_convert_fusion
  3.7 0.3 fusion.4
  4.0 0.1 reshape.101
  4.1 0.3 copy-done.2
  4.5 0.2 reshape.98
  4.8 0.4 fusion.16
  5.2 0.1 fusion.6
  5.5 0.3 fusion.2
  5.9 0.2 reshape.99
  6.1 0.7 pad_maximum_fusion.1.attn_ref
  6.7 0.7 copy.130
  7.4 0.7 pad_maximum_fusion.x_ref
  8.1 0.6 reshape.103.gain_ref
  8.8 0.6 pad.4.blend_ref
  9.4 78.6 %shard_map.145 = bf16[32,1536]{1,0:T(8,128)(2,1)} custom-call(bf16[64,1024]{1,0:T(8,128)(2,1)} %pad_maximum_fusion.1.attn_ref, bf16[2,96,512]{2,1,0:T(8,128)(2,1)} %bitcast.40, bf16[64,1536]{1,0:T(8,128)(2,1)} %pad_maximum_fusion.x_ref, f32[1,1536]{1,0:T(1,128)} %reshape.103.gain_ref, f32[8,128]{1,0:T(8,128)} %pad.4.blend_ref, ...), custom_call_target="tpu_custom_call" | custom-call | tf_op jit(solution)/shard_map/pallas_call | solution.py:559
  88.0 1.5 %copy.132 = bf16[32,1536]{1,0:T(8,128)(2,1)} copy(bf16[32,1536]{1,0:T(8,128)(2,1)} %shard_map.145) | data formatting | bytes 196608
  (47 shorter events, 1.1 us)
Async XLA Ops:
  0.0 1.3 %copy-start.6 = (bf16[8,1024]{1,0:T(8,128)(2,1)S(1)}, bf16[8,1024]{1,0:T(8,128)(2,1)}, u32[]{:S(2)}) copy-start(bf16[8,1024]{1,0:T(8,128)(2,1)} %param.19) | copy-start | bytes 49156
  0.0 1.6 %copy-start.10 = (s32[8]{0:T(128)S(1)}, s32[8]{0:T(128)}, u32[]{:S(2)}) copy-start(s32[8]{0:T(128)} %param.22) | copy-start | bytes 100
  0.0 2.0 %copy-start.8 = (bf16[2,8,128]{2,1,0:T(8,128)(2,1)S(1)}, bf16[2,8,128]{2,1,0:T(8,128)(2,1)}, u32[]{:S(2)}) copy-start(bf16[2,8,128]{2,1,0:T(8,128)(2,1)} %param.20) | copy-start | bytes 12292
  0.0 2.2 %copy-start.11 = (f32[16]{0:T(128)S(1)}, f32[16]{0:T(128)}, u32[]{:S(2)}) copy-start(f32[16]{0:T(128)} %param.23) | copy-start | bytes 196
  3.6 0.9 %copy-start.2 = (bf16[56,1024]{1,0:T(8,128)(2,1)S(1)}, bf16[56,1024]{1,0:T(8,128)(2,1)}, u32[]{:S(2)}) copy-start(bf16[56,1024]{1,0:T(8,128)(2,1)} %param.17) | copy-start | bytes 344068
  3.6 1.1 %copy-start.3 = (bf16[2,56,128]{2,1,0:T(8,128)(2,1)S(1)}, bf16[2,56,128]{2,1,0:T(8,128)(2,1)}, u32[]{:S(2)}) copy-start(bf16[2,56,128]{2,1,0:T(8,128)(2,1)} %param.18) | copy-start | bytes 86020
  5.5 1.2 %copy-start = (bf16[1024,96]{0,1:T(8,128)(2,1)S(1)}, bf16[1024,96]{0,1:T(8,128)(2,1)}, u32[]{:S(2)}) copy-start(bf16[1024,96]{0,1:T(8,128)(2,1)} %param.24) | copy-start | bytes 589828
  5.8 1.6 %copy-start.1 = (bf16[56,1536]{1,0:T(8,128)(2,1)S(1)}, bf16[56,1536]{1,0:T(8,128)(2,1)}, u32[]{:S(2)}) copy-start(bf16[56,1536]{1,0:T(8,128)(2,1)} %param.15) | copy-start | bytes 516100
  5.8 1.6 %copy-start.4 = (bf16[8,1536]{1,0:T(8,128)(2,1)S(1)}, bf16[8,1536]{1,0:T(8,128)(2,1)}, u32[]{:S(2)}) copy-start(bf16[8,1536]{1,0:T(8,128)(2,1)} %param.16) | copy-start | bytes 73732
  5.8 2.3 %copy-start.7 = (f32[1536]{0:T(1024)S(1)}, f32[1536]{0:T(1024)}, u32[]{:S(2)}) copy-start(f32[1536]{0:T(1024)} %param.25) | copy-start | bytes 18436
  5.8 2.9 %copy-start.5 = (f32[64,4]{0,1:T(4,128)S(1)}, f32[64,4]{0,1:T(4,128)}, u32[]{:S(2)}) copy-start(f32[64,4]{0,1:T(4,128)} %param.27) | copy-start | bytes 3076
  5.8 2.9 %copy-start.9 = (s32[64,4]{0,1:T(4,128)S(1)}, s32[64,4]{0,1:T(4,128)}, u32[]{:S(2)}) copy-start(s32[64,4]{0,1:T(4,128)} %param.26) | copy-start | bytes 3076
